TPU v7x, 256 devices: a 4x2x16 block of a 4x16x16 slice. The times are simulated.
256 devices in a mesh: groups: 2 (over y), ep: 16 (over z), dp: 4 (over x), tp: 2 (over core).
Axes of the slice: x: 4, y: 2, z: 16, core: 2. Of those that a mesh axis runs over, the one named last changes fastest.
The devices are a block of a 4x16x16 slice.
Arguments:
- tokens: bfloat16 [16384, 2048], P(('groups', 'ep', 'dp', 'tp')), parts along dimension 0, may hold values from -6 to 6
- experts_one: int32 [16384, 8], P(('groups', 'ep', 'dp', 'tp')), parts along dimension 0, may hold values from 0 to 63, all different within a row; in each aligned block of 64 rows (0 to 63, 64 to 127, ...) at most 10 rows name the same one
- gates_one: float32 [16384, 8], P(('groups', 'ep', 'dp', 'tp')), parts along dimension 0, may hold values from 0.05 to 0.5
- w_in_one: bfloat16 [64, 2048, 2, 768], P(('ep', 'dp'), None, None, 'tp'), may hold values from -0.125 to 0.125
- w_down_one: bfloat16 [64, 768, 2048], P(('ep', 'dp'), 'tp'), may hold values from -0.21875 to 0.21875
- norm_gain: float32 [2048], replicated, may hold values from 0.5 to 1.5
- experts_two: int32 [16384, 8], P(('groups', 'ep', 'dp', 'tp')), parts along dimension 0, may hold values from 0 to 63, all different within a row; in each aligned block of 64 rows (0 to 63, 64 to 127, ...) at most 10 rows name the same one
- gates_two: float32 [16384, 8], P(('groups', 'ep', 'dp', 'tp')), parts along dimension 0, may hold values from 0.05 to 0.5
- placement_two: int32 [64], replicated, may hold values from 0 to 63, each once
- w_in_two: bfloat16 [64, 2048, 2, 768], P(('ep', 'dp'), None, None, 'tp'), may hold values from -0.125 to 0.125
- w_down_two: bfloat16 [64, 768, 2048], P(('ep', 'dp'), 'tp'), may hold values from -0.21875 to 0.21875
Outputs:
- layer_out: bfloat16 [16384, 2048], P(('groups', 'ep', 'dp', 'tp')), parts along dimension 0
There are 2 independent parts, one for each index of `groups`. A program takes and returns all parts, laid end to end along the dimension named above; an argument that names none is the same for every part. Nothing has to cross between parts.
Inputs may be any that keep to these rules, and one draw needn't show every extreme that they name: `experts_one`: each token names 8 different experts; among the 64 tokens of one device no expert is named more than 10 times, and on some device some expert is named exactly 10 times. `experts_two`: each token names 8 different experts; among the 64 tokens of one device no expert is named more than 10 times, and on some device some expert is named exactly 10 times. `placement_two`: each slot is named by exactly one expert.
All inputs are finite; a program needn't handle non-finite values.
Results may differ from a plain program's by a relative error of at most 0.011.
Values may be sent and summed in bfloat16 or wider, within the bound.
A program may use at most 128 MiB of HBM per device.

v0:
```python
import jax
import jax.numpy as jnp
from jax import lax
from jax.sharding import PartitionSpec as P


def rows_first(arrays, axis, dims):
    turned = [jnp.moveaxis(a, dim, 0) for a, dim in zip(arrays, dims)]
    widths = [t[0].size for t in turned]
    both = jnp.concatenate([t.reshape(-1, w) for t, w in zip(turned, widths)], axis=1)
    result = lax.all_gather(both, axis, axis=0, tiled=True)
    pieces = jnp.split(result, [sum(widths[:k]) for k in range(1, len(widths))], axis=1)
    return tuple(
        (
            jnp.moveaxis(b.reshape(-1, *t.shape[1:]), 0, dim)
            for b, t, dim in zip(pieces, turned, dims)
        )
    )


def capacity(tok_rows, top_count, expert_count):
    return max(2, min(tok_rows, 5 * tok_rows * top_count // (4 * expert_count)))


def pack_rows(rows_in, targets, expert_count, per_slot):
    tok_rows, top_count = targets.shape
    flat_ids = targets.reshape(-1)
    hit_table = (flat_ids[:, None] == jnp.arange(expert_count, dtype=jnp.int32)[None, :]).astype(
        jnp.int32
    )
    before = jnp.cumsum(hit_table, axis=0) - hit_table
    slot_rank = jnp.sum(before * hit_table, axis=1)
    slot_index = flat_ids * per_slot + slot_rank
    source = jnp.arange(tok_rows * top_count, dtype=jnp.int32) // top_count
    owner_row = jnp.zeros((expert_count * per_slot,), jnp.int32).at[slot_index].set(source)
    filled = jnp.zeros((expert_count * per_slot,), jnp.int32).at[slot_index].set(1)
    buffer = jnp.where(filled[:, None] > 0, rows_in[owner_row], jnp.zeros((), rows_in.dtype))
    return (buffer, slot_index)


def to_experts(buffer, expert_count, per_slot):
    row_width = buffer.shape[1]
    sectioned_grid = buffer.reshape(lax.axis_size("ep"), lax.axis_size("dp"), per_slot, row_width)
    arrived = lax.all_to_all(
        lax.all_to_all(sectioned_grid, "dp", split_axis=1, concat_axis=1, tiled=True),
        "ep",
        split_axis=0,
        concat_axis=0,
        tiled=True,
    )
    return arrived.reshape(expert_count * per_slot, row_width)


def to_owners(produced, expert_count, per_slot):
    row_width = produced.shape[1]
    sectioned_grid = produced.reshape(lax.axis_size("ep"), lax.axis_size("dp"), per_slot, row_width)
    returned = lax.all_to_all(
        lax.all_to_all(sectioned_grid, "dp", split_axis=1, concat_axis=1, tiled=True),
        "ep",
        split_axis=0,
        concat_axis=0,
        tiled=True,
    )
    return returned.reshape(expert_count * per_slot, row_width)


def run_expert(received, w_in, w_down):
    row_width = received.shape[1]
    down_local = w_down[0]
    half_width = down_local.shape[0]
    row_count = received.shape[0]
    joined, down_all = rows_first((w_in[0], down_local), "tp", (2, 0))
    full_width = joined.shape[2]
    gate_up = jnp.dot(
        received, joined.reshape(row_width, 2 * full_width), preferred_element_type=jnp.float32
    )
    hidden = (jax.nn.silu(gate_up[:, :full_width]) * gate_up[:, full_width:]).astype(jnp.bfloat16)
    total = jnp.zeros((row_count, row_width), jnp.float32)
    for block in range(lax.axis_size("tp")):
        lo_unit = block * half_width
        partial_out = jnp.dot(
            hidden[:, lo_unit : lo_unit + half_width],
            down_all[lo_unit : lo_unit + half_width],
            preferred_element_type=jnp.float32,
        )
        total = total + partial_out.astype(jnp.bfloat16).astype(jnp.float32)
    return total.astype(jnp.bfloat16)


def moe_block(rows_in, targets, gate_values, w_in, w_down, expert_count, per_slot):
    tok_rows, top_count = targets.shape
    row_width = rows_in.shape[1]
    buffer, slot_index = pack_rows(rows_in, targets, expert_count, per_slot)
    arrived = to_experts(buffer, expert_count, per_slot)
    produced = run_expert(arrived, w_in, w_down)
    returned = to_owners(produced, expert_count, per_slot)
    picked = returned[slot_index].reshape(tok_rows, top_count, row_width)
    return jnp.sum(gate_values[:, :, None] * picked.astype(jnp.float32), axis=1)


def shards(
    tokens,
    experts_one,
    gates_one,
    w_in_one,
    w_down_one,
    norm_gain,
    experts_two,
    gates_two,
    placement_two,
    w_in_two,
    w_down_two,
):
    tok_rows, top_count = experts_one.shape
    expert_count = placement_two.shape[0]
    per_slot = capacity(tok_rows, top_count, expert_count)
    moe_one = moe_block(
        tokens, experts_one, gates_one, w_in_one, w_down_one, expert_count, per_slot
    )
    mixed = (tokens.astype(jnp.float32) + moe_one).astype(jnp.bfloat16)
    mixed = lax.optimization_barrier(mixed)
    mixed_wide = mixed.astype(jnp.float32)
    inv_rms = lax.rsqrt(jnp.mean(mixed_wide * mixed_wide, axis=1, keepdims=True) + 1e-06)
    normed = (mixed_wide * inv_rms * norm_gain[None, :]).astype(jnp.bfloat16)
    expert_range = jnp.arange(expert_count, dtype=jnp.int32)
    matches = experts_two[:, :, None] == expert_range[None, None, :]
    layer_slots = jnp.sum(jnp.where(matches, placement_two[None, None, :], 0), axis=2)
    moe_two = moe_block(
        normed, layer_slots, gates_two, w_in_two, w_down_two, expert_count, per_slot
    )
    return (mixed_wide + moe_two).astype(jnp.bfloat16)


def solution(mesh):
    in_specs = (
        P(("groups", "ep", "dp", "tp"), None),
        P(("groups", "ep", "dp", "tp"), None),
        P(("groups", "ep", "dp", "tp"), None),
        P(("ep", "dp"), None, None, "tp"),
        P(("ep", "dp"), "tp", None),
        P(),
        P(("groups", "ep", "dp", "tp"), None),
        P(("groups", "ep", "dp", "tp"), None),
        P(),
        P(("ep", "dp"), None, None, "tp"),
        P(("ep", "dp"), "tp", None),
    )
    out_specs = P(("groups", "ep", "dp", "tp"), None)
    return jax.shard_map(shards, mesh=mesh, in_specs=in_specs, out_specs=out_specs, check_vma=False)
```

profile of v0, /device:TPU:33, one launch (start us, length us, event | category | flops | bytes accessed | tf_op | source)
XLA Modules:
  0.0 809.1 jit_solution(14812893215207839693)
XLA Ops:
  31.3 6.4 reshape.167
  40.3 9.6 %all-to-all-done = bf16[16,4,10,2048]{3,0,2,1:T(8,128)(2,1)} async-done(((bf16[16,4,10,2048]{3,0,2,1:T(8,128)(2,1)}), bf16[16,4,10,2048]{3,0,2,1:T(8,128)(2,1)}, u32[]{:S(2)}, u32[]{:S(2)}) %all-to-all-start) | async-done | bytes 2621472 | tf_op jit(solution)/shard_map/all_to_all | solution.py:45
  55.2 37.0 %all-to-all-start.1 = ((bf16[16,4,10,2048]{3,1,2,0:T(4,128)(2,1)}), bf16[16,4,10,2048]{3,1,2,0:T(4,128)(2,1)}, u32[]{:S(2)}, u32[]{:S(2)}) async-start(bf16[16,4,10,2048]{3,1,2,0:T(4,128)(2,1)} %copy.61), calls=%async_computation.1 | async-start | bytes 5242880 | tf_op jit(solution)/shard_map/all_to_all | solution.py:44
  96.4 32.5 %all-gather.3.cloned.1.call-done = bf16[768,6144]{0,1:T(8,128)(2,1)} async-done(((bf16[384,6144]{0,1:T(8,128)(2,1)}), bf16[768,6144]{0,1:T(8,128)(2,1)}) %all-gather.3.cloned.1.call-update) | async-done | bytes 9437200 | tf_op jit(solution)/shard_map/all_gather | solution.py:11
  128.9 5.9 split.10
  134.8 13.5 %reshape.168 = bf16[768,2048,2]{0,2,1:T(2,128)(2,1)} reshape(bf16[768,4096]{0,1:T(8,128)(2,1)} %split.10) | data formatting | bytes 12582912 | tf_op jit(solution)/shard_map/reshape | solution.py:15
  148.3 6.8 copy.79
  155.1 51.1 %all-to-all-done.1 = bf16[16,4,10,2048]{3,1,2,0:T(4,128)(2,1)} async-done(((bf16[16,4,10,2048]{3,1,2,0:T(4,128)(2,1)}), bf16[16,4,10,2048]{3,1,2,0:T(4,128)(2,1)}, u32[]{:S(2)}, u32[]{:S(2)}) %all-to-all-start.1) | async-done | bytes 2621472 | tf_op jit(solution)/shard_map/all_to_all | solution.py:44
  216.0 6.3 fusion.35
  235.4 30.5 %all_to_all.40 = bf16[16,4,10,2048]{3,0,2,1:T(8,128)(2,1)S(1)} all-to-all(bf16[16,4,10,2048]{3,0,2,1:T(8,128)(2,1)S(1)} %copy.64), channel_id=1, replica_groups=mesh['groups'=2,'ep'=16,'dp'=4,'tp'=2] {'dp'}, dimensions={1} | all-to-all | bytes 5242880 | tf_op jit(solution)/shard_map/all_to_all | solution.py:58
  269.4 15.6 %all-to-all-start.3 = ((bf16[16,4,10,2048]{3,1,2,0:T(4,128)(2,1)}), bf16[16,4,10,2048]{3,1,2,0:T(4,128)(2,1)S(1)}, u32[]{:S(2)}, u32[]{:S(2)}) async-start(bf16[16,4,10,2048]{3,1,2,0:T(4,128)(2,1)} %copy.65), calls=%async_computation.3 | async-start | bytes 5242880 | tf_op jit(solution)/shard_map/all_to_all | solution.py:57
  293.5 105.4 %all-to-all-done.3 = bf16[16,4,10,2048]{3,1,2,0:T(4,128)(2,1)S(1)} async-done(((bf16[16,4,10,2048]{3,1,2,0:T(4,128)(2,1)}), bf16[16,4,10,2048]{3,1,2,0:T(4,128)(2,1)S(1)}, u32[]{:S(2)}, u32[]{:S(2)}) %all-to-all-start.3) | async-done | bytes 2621472 | tf_op jit(solution)/shard_map/all_to_all | solution.py:57
  431.1 6.4 reshape.174
  440.1 18.3 %all-to-all-done.4 = bf16[16,4,10,2048]{3,0,2,1:T(8,128)(2,1)} async-done(((bf16[16,4,10,2048]{3,0,2,1:T(8,128)(2,1)}), bf16[16,4,10,2048]{3,0,2,1:T(8,128)(2,1)}, u32[]{:S(2)}, u32[]{:S(2)}) %all-to-all-start.4) | async-done | bytes 2621472 | tf_op jit(solution)/shard_map/all_to_all | solution.py:45
  463.7 15.9 %all-to-all-start.5 = ((bf16[16,4,10,2048]{3,1,2,0:T(4,128)(2,1)}), bf16[16,4,10,2048]{3,1,2,0:T(4,128)(2,1)}, u32[]{:S(2)}, u32[]{:S(2)}) async-start(bf16[16,4,10,2048]{3,1,2,0:T(4,128)(2,1)} %copy.71), calls=%async_computation.5 | async-start | bytes 5242880 | tf_op jit(solution)/shard_map/all_to_all | solution.py:44
  483.9 32.5 %all-gather.5.cloned.1.call-done = bf16[768,6144]{0,1:T(8,128)(2,1)} async-done(((bf16[384,6144]{0,1:T(8,128)(2,1)}), bf16[768,6144]{0,1:T(8,128)(2,1)}) %all-gather.5.cloned.1.call-update) | async-done | bytes 9437200 | tf_op jit(solution)/shard_map/all_gather | solution.py:11
  516.4 5.9 split.11
  522.3 13.5 %reshape.175 = bf16[768,2048,2]{0,2,1:T(2,128)(2,1)} reshape(bf16[768,4096]{0,1:T(8,128)(2,1)} %split.11) | data formatting | bytes 12582912 | tf_op jit(solution)/shard_map/reshape | solution.py:15
  535.8 6.8 copy.80
  542.6 51.0 %all-to-all-done.5 = bf16[16,4,10,2048]{3,1,2,0:T(4,128)(2,1)} async-done(((bf16[16,4,10,2048]{3,1,2,0:T(4,128)(2,1)}), bf16[16,4,10,2048]{3,1,2,0:T(4,128)(2,1)}, u32[]{:S(2)}, u32[]{:S(2)}) %all-to-all-start.5) | async-done | bytes 2621472 | tf_op jit(solution)/shard_map/all_to_all | solution.py:44
  603.4 6.3 fusion.36
  622.8 30.0 %all_to_all.41 = bf16[16,4,10,2048]{3,0,2,1:T(8,128)(2,1)S(1)} all-to-all(bf16[16,4,10,2048]{3,0,2,1:T(8,128)(2,1)S(1)} %copy.74), channel_id=1, replica_groups=mesh['groups'=2,'ep'=16,'dp'=4,'tp'=2] {'dp'}, dimensions={1} | all-to-all | bytes 5242880 | tf_op jit(solution)/shard_map/all_to_all | solution.py:58
  656.3 16.0 %all-to-all-start.7 = ((bf16[16,4,10,2048]{3,1,2,0:T(4,128)(2,1)}), bf16[16,4,10,2048]{3,1,2,0:T(4,128)(2,1)S(1)}, u32[]{:S(2)}, u32[]{:S(2)}) async-start(bf16[16,4,10,2048]{3,1,2,0:T(4,128)(2,1)} %copy.75), calls=%async_computation.7 | async-start | bytes 5242880 | tf_op jit(solution)/shard_map/all_to_all | solution.py:57
  672.5 113.7 %all-to-all-done.7 = bf16[16,4,10,2048]{3,1,2,0:T(4,128)(2,1)S(1)} async-done(((bf16[16,4,10,2048]{3,1,2,0:T(4,128)(2,1)}), bf16[16,4,10,2048]{3,1,2,0:T(4,128)(2,1)S(1)}, u32[]{:S(2)}, u32[]{:S(2)}) %all-to-all-start.7) | async-done | bytes 2621472 | tf_op jit(solution)/shard_map/all_to_all | solution.py:57
  (108 shorter events, 157.9 us)
Async XLA Ops:
  6.5 5.2 copy-start
  26.1 23.7 %all-to-all-start = ((bf16[16,4,10,2048]{3,0,2,1:T(8,128)(2,1)}), bf16[16,4,10,2048]{3,0,2,1:T(8,128)(2,1)}, u32[]{:S(2)}, u32[]{:S(2)}) async-start(bf16[16,4,10,2048]{3,0,2,1:T(8,128)(2,1)} %copy.60), calls=%async_computation | async-start | bytes 5242880 | tf_op jit(solution)/shard_map/all_to_all | solution.py:45
  55.2 151.0 %all-to-all-start.1 = ((bf16[16,4,10,2048]{3,1,2,0:T(4,128)(2,1)}), bf16[16,4,10,2048]{3,1,2,0:T(4,128)(2,1)}, u32[]{:S(2)}, u32[]{:S(2)}) async-start(bf16[16,4,10,2048]{3,1,2,0:T(4,128)(2,1)} %copy.61), calls=%async_computation.1 | async-start | bytes 5242880 | tf_op jit(solution)/shard_map/all_to_all | solution.py:44
  92.2 36.8 %all-gather.3.cloned.1.call-start = ((), (), s32[]{:S(2)}) async-start(), calls=%async_computation.8 | async-start | bytes 14155776 | tf_op jit(solution)/shard_map/all_gather | solution.py:11
  269.4 15.7 %copy-start.4 = (s32[64,8]{0,1:T(8,128)S(1)}, s32[64,8]{0,1:T(8,128)}, u32[]{:S(2)}) copy-start(s32[64,8]{0,1:T(8,128)} %param.17) | copy-start | bytes 6148
  269.4 15.8 %copy-start.7 = (s32[64]{0:T(128)S(1)}, s32[64]{0:T(128)}, u32[]{:S(2)}) copy-start(s32[64]{0:T(128)} %param.19) | copy-start | bytes 772
  269.4 23.8 %copy-start.5 = (f32[64,8]{0,1:T(8,128)S(1)}, f32[64,8]{0,1:T(8,128)}, u32[]{:S(2)}) copy-start(f32[64,8]{0,1:T(8,128)} %param.13) | copy-start | bytes 6148
  269.4 129.5 %all-to-all-start.3 = ((bf16[16,4,10,2048]{3,1,2,0:T(4,128)(2,1)}), bf16[16,4,10,2048]{3,1,2,0:T(4,128)(2,1)S(1)}, u32[]{:S(2)}, u32[]{:S(2)}) async-start(bf16[16,4,10,2048]{3,1,2,0:T(4,128)(2,1)} %copy.65), calls=%async_computation.3 | async-start | bytes 5242880 | tf_op jit(solution)/shard_map/all_to_all | solution.py:57
  410.4 4.2 copy-start.3
  413.9 0.7 copy-start.1
  426.5 31.9 %all-to-all-start.4 = ((bf16[16,4,10,2048]{3,0,2,1:T(8,128)(2,1)}), bf16[16,4,10,2048]{3,0,2,1:T(8,128)(2,1)}, u32[]{:S(2)}, u32[]{:S(2)}) async-start(bf16[16,4,10,2048]{3,0,2,1:T(8,128)(2,1)} %copy.70), calls=%async_computation.4 | async-start | bytes 5242880 | tf_op jit(solution)/shard_map/all_to_all | solution.py:45
  463.7 129.9 %all-to-all-start.5 = ((bf16[16,4,10,2048]{3,1,2,0:T(4,128)(2,1)}), bf16[16,4,10,2048]{3,1,2,0:T(4,128)(2,1)}, u32[]{:S(2)}, u32[]{:S(2)}) async-start(bf16[16,4,10,2048]{3,1,2,0:T(4,128)(2,1)} %copy.71), calls=%async_computation.5 | async-start | bytes 5242880 | tf_op jit(solution)/shard_map/all_to_all | solution.py:44
  479.7 36.8 %all-gather.5.cloned.1.call-start = ((), (), s32[]{:S(2)}) async-start(), calls=%async_computation.9 | async-start | bytes 14155776 | tf_op jit(solution)/shard_map/all_gather | solution.py:11
  656.3 16.0 %copy-start.6 = (f32[64,8]{0,1:T(8,128)S(1)}, f32[64,8]{0,1:T(8,128)}, u32[]{:S(2)}) copy-start(f32[64,8]{0,1:T(8,128)} %param.18) | copy-start | bytes 6148
  656.3 129.9 %all-to-all-start.7 = ((bf16[16,4,10,2048]{3,1,2,0:T(4,128)(2,1)}), bf16[16,4,10,2048]{3,1,2,0:T(4,128)(2,1)S(1)}, u32[]{:S(2)}, u32[]{:S(2)}) async-start(bf16[16,4,10,2048]{3,1,2,0:T(4,128)(2,1)} %copy.75), calls=%async_computation.7 | async-start | bytes 5242880 | tf_op jit(solution)/shard_map/all_to_all | solution.py:57
  797.6 3.5 copy-start.2
Sparse Core Ops, SparseCore 0:
  96.6 32.3 all-gather.2
  484.0 32.3 all-gather.4
where the time goes:
time: 823 us; the launch traced here: 809 us
  waiting for transfers between devices  414 us (50%)
  local copies, waits for them, and re-layouts  175 us (21%)
  starting transfers between devices  94.5 us (11%)
  blocking collectives  60.6 us (7%)
  other arithmetic  26.6 us (3%)
  matrix products  24.5 us (3%)
  between operations  14.3 us (2%)
    all_to_all x2, waiting for transfers between devices, to_owners(): lax.all_to_all(lax.all_to_all(sectioned_grid, 'dp', split_axis=1, concat_...  219 us
    all_to_all x2, waiting for transfers between devices, to_experts(): lax.all_to_all(lax.all_to_all(sectioned_grid, 'dp', split_axis=1, concat_...  102 us
    all_gather x2, waiting for transfers between devices, rows_first(): result = lax.all_gather(both, axis, axis=0, tiled=True)  65 us
    all_to_all x2, blocking collectives, to_owners(): lax.all_to_all(sectioned_grid, 'dp', split_axis=1, concat_axis=1, tiled=T...  60.6 us
    all_to_all x2, starting transfers between devices, to_experts(): lax.all_to_all(lax.all_to_all(sectioned_grid, 'dp', split_axis=1, concat_...  52.9 us
    all_to_all x2, starting transfers between devices, to_owners(): lax.all_to_all(lax.all_to_all(sectioned_grid, 'dp', split_axis=1, concat_...  31.7 us
    all_to_all x2, waiting for transfers between devices, to_experts(): lax.all_to_all(sectioned_grid, 'dp', split_axis=1, concat_axis=1, tiled=T...  27.8 us
    reshape x2, local copies, waits for them, and re-layouts, rows_first(): b.reshape(-1, *t.shape[1:])  26.9 us
  transfers between devices with their start and end apart: 8, of which 8 were waited for; matrix products, arithmetic and copies ran while one was open for 11% of the time, Pallas kernels for 0%

commit v1 on v0

v1 whole, which is shorter than its diff:
```python
import functools

import jax
import jax.numpy as jnp
from jax import lax
from jax.experimental import pallas as pl
from jax.experimental.pallas import tpu as pltpu
from jax.sharding import PartitionSpec as P

F32, BF16 = jnp.float32, jnp.bfloat16
MESH = pl.DeviceIdType.MESH
PIECES = 4


def capacity(tok_rows, top_count, expert_count):
    return max(2, min(tok_rows, 5 * tok_rows * top_count // (4 * expert_count)))


def layer_kernel(dims, with_norm, *refs):
    nz, nx, tok, width, half_ff, top, cap, rows = dims
    steps = nz // 2
    pr = tok // PIECES
    slab = nx * rows
    refs = list(refs)
    rows_ref, meta_ref, w_in, w_down = refs[:4]
    refs = refs[4:]
    if with_norm:
        gain_ref, mixed_ref, normed_ref = refs[:3]
        resid_ref = rows_ref
        refs = refs[3:]
    else:
        resid_ref, out_ref = refs[:2]
        refs = refs[2:]
    (ag, m_right, m_left, ct, snd, recv, hid, outs, back, rs_right, rs_left, contrib, own,
     wi, wd, ag_s, ag_r, m_s, m_r, x_s, x_r, b_s, b_r, rs_s, rs_r, w_s, w_r, w_l) = refs

    z, x, c = lax.axis_index("ep"), lax.axis_index("dp"), lax.axis_index("tp")
    right, left = lax.rem(z + 1, nz), lax.rem(z + nz - 1, nz)
    peers = [lax.rem(x + k, nx) for k in range(nx)]

    def to(axis, index):
        return {axis: index}

    barrier = pltpu.get_barrier_semaphore()
    pl.semaphore_signal(barrier, inc=1, device_id=to("tp", 1 - c), device_id_type=MESH)
    for index in (right, left):
        pl.semaphore_signal(barrier, inc=1, device_id=to("ep", index), device_id_type=MESH)
    for k in range(1, nx):
        pl.semaphore_signal(barrier, inc=1, device_id=to("dp", peers[k]), device_id_type=MESH)
    pl.semaphore_wait(barrier, 2 + nx)

    def remote(src, dst, send, recv_sem, axis, index):
        return pltpu.make_async_remote_copy(
            src_ref=src, dst_ref=dst, send_sem=send, recv_sem=recv_sem,
            device_id=to(axis, index), device_id_type=MESH,
        )

    def cut(p, base=0):
        return pl.ds(base + p * pr, pr)

    def ring_copy(src, s, p, way):
        if way == 0:
            dst = ag.at[s, cut(p)]
        else:
            dst = ag.at[s, pl.ds(pl.multiple_of(jnp.where(s == steps, p * pr, tok + p * pr), pr), pr)]
        return remote(src, dst, ag_s.at[way, s, p], ag_r.at[way, s, p], "ep", (right, left)[way])

    def ring_block(s, p, way):
        if way == 0:
            return ag.at[s, cut(p)]
        return ag.at[s, cut(p, tok)]

    def meta_copy(src, s, way):
        return remote(src, (m_right, m_left)[way].at[s], m_s.at[way, s], m_r.at[way, s], "ep", (right, left)[way])

    for p in range(PIECES):
        for way in (0, 1):
            ring_copy(rows_ref.at[cut(p)], jnp.int32(1), p, way).start()
        if p == 0:
            for way in (0, 1):
                meta_copy(meta_ref, 1, way).start()

    mine = [
        pltpu.make_async_copy(w_in, wi.at[0], w_l.at[0]),
        pltpu.make_async_copy(w_down, wd.at[0], w_l.at[1]),
    ]
    other = [
        remote(w_in, wi.at[1], w_s.at[0], w_r.at[0], "tp", 1 - c),
        remote(w_down, wd.at[1], w_s.at[1], w_r.at[1], "tp", 1 - c),
    ]
    for k in (0, 1):
        other[k].start()
        mine[k].start()

    ag[steps, pl.ds(tok, tok)] = rows_ref[...]
    m_left[steps] = meta_ref[...]
    quiet = tok // 2
    rs_right[1, pl.ds(quiet, tok - quiet)] = jnp.zeros((tok - quiet, width), BF16)
    rs_left[1, pl.ds(0, quiet)] = jnp.zeros((quiet, width), BF16)

    lane = lax.broadcasted_iota(jnp.int32, (8, 2 * tok), 1)
    first = (z * nx).astype(F32)

    def select(s):
        info = jnp.concatenate([m_right[s][:, :tok], m_left[s][:, :tok]], axis=1)
        ids, gates = info[:top], info[top:]
        hits, values = [], []
        for k in range(nx):
            hit = ids == first + k
            hits.append(jnp.sum(jnp.where(hit, 1.0, 0.0), axis=0, keepdims=True))
            values.append(jnp.sum(jnp.where(hit, gates, 0.0), axis=0, keepdims=True))
        hit_all = jnp.concatenate(hits + [jnp.zeros((8 - nx, 2 * tok), F32)], axis=0)
        a = lax.broadcasted_iota(jnp.int32, (2 * tok, 2 * tok), 0)
        b = lax.broadcasted_iota(jnp.int32, (2 * tok, 2 * tok), 1)
        before = jnp.where((a < b) & ((a >= tok) == (b >= tok)), 1.0, 0.0).astype(BF16)
        rank = jnp.dot(hit_all.astype(BF16), before, preferred_element_type=F32)
        code = jnp.where(hit_all > 0.5, rank + jnp.where(lane >= tok, float(cap), 0.0), -1.0)
        place = lax.broadcasted_iota(jnp.int32, (rows, 2 * tok), 0).astype(F32)
        ones, weights = [], []
        for k in range(nx):
            pick = jnp.where(place == code[k:k + 1], 1.0, 0.0)
            ones.append(pick)
            weights.append(pick * values[k])
        pick = jnp.concatenate(ones, axis=0).astype(BF16)
        weight = jnp.concatenate(weights, axis=0)
        high = weight.astype(BF16)
        ct[s] = jnp.concatenate([high, (weight - high.astype(F32)).astype(BF16)], axis=1)
        chosen = jnp.dot(pick, ag[s], preferred_element_type=F32).astype(BF16)
        snd[s] = chosen.reshape(nx, rows, width)
        for k in range(1, nx):
            to_expert(s, k).start()
        recv[s, x] = snd[s, x]

    def to_expert(s, k):
        return remote(snd.at[s, peers[k]], recv.at[s, x], x_s.at[s, k], x_r.at[s, k], "dp", peers[k])

    def from_owner(s, k):
        source = lax.rem(x + nx - k, nx)
        return remote(snd.at[s, source], recv.at[s, source], x_s.at[s, k], x_r.at[s, k], "dp", peers[k])

    def to_owner(s, k):
        return remote(outs.at[s, peers[k]], back.at[s, x], b_s.at[s, k], b_r.at[s, k], "dp", peers[k])

    def from_expert(s, k):
        source = lax.rem(x + nx - k, nx)
        return remote(outs.at[s, source], back.at[s, source], b_s.at[s, k], b_r.at[s, k], "dp", peers[k])

    def hidden(s, h):
        got = recv[s].reshape(slab, width)
        both = jnp.dot(got, wi[h], preferred_element_type=F32)
        gate, up = both[:, :half_ff], both[:, half_ff:]
        hid[h] = (gate * (1.0 / (1.0 + jnp.exp(-gate))) * up).astype(BF16)

    def down(s):
        parts = [jnp.dot(hid[h], wd[h], preferred_element_type=F32).astype(BF16).astype(F32) for h in (0, 1)]
        outs[s] = (parts[0] + parts[1]).astype(BF16).reshape(nx, rows, width)
        back[s, x] = outs[s, x]

    def gather_step(s, carry):
        for p in range(PIECES):
            moving = s <= steps - 1
            here = [moving | ((s == steps) & (p < PIECES // 2)), moving | ((s == steps) & (p >= PIECES // 2))]
            onward = [(s < steps - 1) | ((s == steps - 1) & (p < PIECES // 2)),
                      (s < steps - 1) | ((s == steps - 1) & (p >= PIECES // 2))]
            for way in (0, 1):
                @pl.when(here[way])
                def _():
                    ring_copy(ring_block(1, p, way), s, p, way).wait_recv()

                @pl.when(onward[way])
                def _():
                    ring_copy(ring_block(s, p, way), s + 1, p, way).start()
            if p == 0:
                @pl.when(s <= steps)
                def _():
                    meta_copy(meta_ref, s, 0).wait_recv()

                @pl.when(moving)
                def _():
                    meta_copy(meta_ref, s, 1).wait_recv()
                    meta_copy(m_right.at[s], s + 1, 0).start()

                @pl.when(s < steps - 1)
                def _():
                    meta_copy(m_left.at[s], s + 1, 1).start()

                @pl.when((s >= 2) & (s <= steps + 1))
                def _():
                    select(s - 1)
            if p == 1:
                @pl.when(s == 3)
                def _():
                    for k in (0, 1):
                        mine[k].wait()
                        other[k].wait()

                @pl.when(s >= 3)
                def _():
                    for k in range(1, nx):
                        from_owner(s - 2, k).wait_recv()
                    hidden(s - 2, 0)
            if p == 2:
                @pl.when(s >= 3)
                def _():
                    hidden(s - 2, 1)
            if p == 3:
                @pl.when(s >= 3)
                def _():
                    down(s - 2)

                @pl.when(s >= steps + 1)
                def _():
                    for k in range(1, nx):
                        to_owner(s - 2, k).start()
        return carry

    lax.fori_loop(1, steps + 3, gather_step, 0)

    def return_rest(i, carry):
        for k in range(1, nx):
            to_owner(steps - 2 - i, k).start()
        return carry

    lax.fori_loop(0, steps - 2, return_rest, 0)

    def scatter_copy(src, j, p, way):
        dst = (rs_right, rs_left)[way].at[j, cut(p)]
        return remote(src, dst, rs_s.at[way, j, p], rs_r.at[way, j, p], "ep", (right, left)[way])

    def combine(s):
        for k in range(1, nx):
            from_expert(s, k).wait_recv()
        both = lax.dot_general(ct[s], back[s].reshape(slab, width), (((0,), (0,)), ((), ())),
                               preferred_element_type=F32)
        contrib[...] = both[:2 * tok] + both[2 * tok:]

    combine(steps)
    for p in range(PIECES):
        way = 0 if p < PIECES // 2 else 1
        buf = (rs_right, rs_left)[way]
        buf[0, cut(p)] = contrib[cut(p)].astype(BF16)
        scatter_copy(buf.at[0, cut(p)], 1, p, way).start()
    own[...] = contrib[pl.ds(tok, tok)]

    def scatter_step(j, carry):
        combine(steps - j)
        for p in range(PIECES):
            for way in (0, 1):
                buf = (rs_right, rs_left)[way]

                @pl.when((j >= 2) | ((p < PIECES // 2) == (way == 0)))
                def _():
                    scatter_copy(buf.at[0, cut(p)], j, p, way).wait_recv()

                part = contrib[cut(p, tok if way == 0 else 0)]
                buf[j, cut(p)] = (buf[j, cut(p)].astype(F32) + part).astype(BF16)
                scatter_copy(buf.at[j, cut(p)], j + 1, p, way).start()
        return carry

    lax.fori_loop(1, steps, scatter_step, 0)

    for p in range(PIECES):
        for way in (0, 1):
            buf = (rs_right, rs_left)[way]
            scatter_copy(buf.at[0, cut(p)], steps, p, way).wait_recv()
        total = own[cut(p)] + rs_right[steps, cut(p)].astype(F32) + rs_left[steps, cut(p)].astype(F32)
        mixed = (resid_ref[cut(p)].astype(F32) + total).astype(BF16)
        if with_norm:
            mixed_ref[cut(p)] = mixed
            wide = mixed.astype(F32)
            scale = lax.rsqrt(jnp.mean(wide * wide, axis=1, keepdims=True) + 1e-06)
            normed_ref[cut(p)] = (wide * scale * gain_ref[...]).astype(BF16)
        else:
            out_ref[cut(p)] = mixed

    def sent(s, carry):
        for p in range(PIECES):
            for way in (0, 1):
                @pl.when((s < steps) | ((p < PIECES // 2) == (way == 0)))
                def _():
                    ring_copy(ring_block(1, p, way), s, p, way).wait_send()

                @pl.when((s > 1) | ((p < PIECES // 2) == (way == 0)))
                def _():
                    scatter_copy((rs_right, rs_left)[way].at[0, cut(p)], s, p, way).wait_send()
        meta_copy(meta_ref, s, 0).wait_send()

        @pl.when(s < steps)
        def _():
            meta_copy(meta_ref, s, 1).wait_send()
        for k in range(1, nx):
            to_expert(s, k).wait_send()
            to_owner(s, k).wait_send()
        return carry

    lax.fori_loop(1, steps + 1, sent, 0)


def moe_layer(sizes, cap, with_norm, collective_id, rows_in, meta, w_in, w_down, extra):
    nz, nx = sizes
    tok, width = rows_in.shape
    half_ff = w_down.shape[0]
    top = meta.shape[0] // 2
    rows = -(-2 * cap // 16) * 16
    dims = (nz, nx, tok, width, half_ff, top, cap, rows)
    groups = nz // 2 + 1
    dma = pltpu.SemaphoreType.DMA
    vmem, hbm = pl.BlockSpec(memory_space=pltpu.VMEM), pl.BlockSpec(memory_space=pl.ANY)
    shape = jax.ShapeDtypeStruct((tok, width), BF16)
    scratch = [
        pltpu.VMEM((groups, 2 * tok, width), BF16),
        pltpu.VMEM((groups, *meta.shape), F32),
        pltpu.VMEM((groups, *meta.shape), F32),
        pltpu.VMEM((groups, nx * rows, 4 * tok), BF16),
        pltpu.VMEM((groups, nx, rows, width), BF16),
        pltpu.VMEM((groups, nx, rows, width), BF16),
        pltpu.VMEM((2, nx * rows, half_ff), BF16),
        pltpu.VMEM((groups, nx, rows, width), BF16),
        pltpu.VMEM((groups, nx, rows, width), BF16),
        pltpu.VMEM((groups, tok, width), BF16),
        pltpu.VMEM((groups, tok, width), BF16),
        pltpu.VMEM((2 * tok, width), F32),
        pltpu.VMEM((tok, width), F32),
        pltpu.VMEM((2, width, 2 * half_ff), BF16),
        pltpu.VMEM((2, half_ff, width), BF16),
        dma((2, groups, PIECES)),
        dma((2, groups, PIECES)),
        dma((2, groups)),
        dma((2, groups)),
        dma((groups, nx)),
        dma((groups, nx)),
        dma((groups, nx)),
        dma((groups, nx)),
        dma((2, groups, PIECES)),
        dma((2, groups, PIECES)),
        dma((2,)),
        dma((2,)),
        dma((2,)),
    ]
    return pl.pallas_call(
        functools.partial(layer_kernel, dims, with_norm),
        out_shape=(shape, shape) if with_norm else shape,
        in_specs=[vmem, vmem, hbm, hbm, vmem],
        out_specs=(vmem, vmem) if with_norm else vmem,
        scratch_shapes=scratch,
        compiler_params=pltpu.CompilerParams(
            collective_id=collective_id, has_side_effects=True, vmem_limit_bytes=60 * 1024 * 1024
        ),
        name="moe_norm" if with_norm else "moe_last",
    )(rows_in, meta, w_in, w_down, extra)


def routing(ids, gates):
    wide = jnp.concatenate([ids.T.astype(F32), gates.T], axis=0)
    return jnp.pad(wide, ((0, 0), (0, -wide.shape[1] % 128)))


def shards(sizes, tokens, experts_one, gates_one, w_in_one, w_down_one, norm_gain,
           experts_two, gates_two, placement_two, w_in_two, w_down_two):
    tok_rows, top_count = experts_one.shape
    expert_count = placement_two.shape[0]
    cap = capacity(tok_rows, top_count, expert_count)
    expert_range = jnp.arange(expert_count, dtype=jnp.int32)
    matches = experts_two[:, :, None] == expert_range[None, None, :]
    slots_two = jnp.sum(jnp.where(matches, placement_two[None, None, :], 0), axis=2)

    def flat(w):
        return w[0].reshape(w.shape[1], w.shape[2] * w.shape[3])

    mixed, normed = moe_layer(sizes, cap, True, 0, tokens, routing(experts_one, gates_one),
                              flat(w_in_one), w_down_one[0], norm_gain[None, :])
    return moe_layer(sizes, cap, False, 1, normed, routing(slots_two, gates_two),
                     flat(w_in_two), w_down_two[0], mixed)


def solution(mesh):
    own = P(("groups", "ep", "dp", "tp"), None)
    w_in, w_down = P(("ep", "dp"), None, None, "tp"), P(("ep", "dp"), "tp", None)
    in_specs = (own, own, own, w_in, w_down, P(), own, own, P(), w_in, w_down)
    sizes = (mesh.shape["ep"], mesh.shape["dp"])
    return jax.shard_map(functools.partial(shards, sizes), mesh=mesh, in_specs=in_specs, out_specs=own,
                         check_vma=False)
```

time: 823 us -> 282 us (0.34); the launches traced: 809 us -> 277 us
  waiting for transfers between devices: 414 us -> 0 us
  Pallas kernels: 0 us -> 263 us
  local copies, waits for them, and re-layouts: 175 us -> 9 us
  starting transfers between devices: 94.5 us -> 0 us
  blocking collectives: 60.6 us -> 0 us
  matrix products: 24.5 us -> 0 us
  other arithmetic: 26.6 us -> 5.17 us
  between operations: 14.3 us -> 0.03 us
    all_to_all x6 -> x0, waiting for transfers between devices: 349 us -> none  [the longest x2 219 us: to_owners(): lax.all_to_all(lax.all_to_all(sectioned_grid, 'dp', split_axis=1, concat_...]
    pallas_call x0 -> x2, Pallas kernels: none -> 263 us  [moe_layer(): pl.pallas_call(functools.partial(layer_kernel, dims, with_norm), out_shap...]
    all_to_all x6 -> x0, starting transfers between devices: 94.3 us -> none  [the longest x2 52.9 us: to_experts(): lax.all_to_all(lax.all_to_all(sectioned_grid, 'dp', split_axis=1, concat_...]
    reshape x12 -> x0, local copies, waits for them, and re-layouts: 69.1 us -> none  [the longest x2 26.9 us: rows_first(): b.reshape(-1, *t.shape[1:])]
    all_gather x2 -> x0, waiting for transfers between devices: 65 us -> none  [rows_first(): result = lax.all_gather(both, axis, axis=0, tiled=True)]
    all_to_all x2 -> x0, blocking collectives: 60.6 us -> none  [to_owners(): lax.all_to_all(sectioned_grid, 'dp', split_axis=1, concat_axis=1, tiled=T...]
    all_to_all x8 -> x0, local copies, waits for them, and re-layouts: 37 us -> none  [the longest x2 11.4 us: to_experts(): lax.all_to_all(lax.all_to_all(sectioned_grid, 'dp', split_axis=1, concat_...]
    dot_general x6 -> x0, matrix products: 24.5 us -> none  [the longest x2 12.6 us: run_expert(): jnp.dot(received, joined.reshape(row_width, 2 * full_width), preferred_el...]
  transfers between devices with their start and end apart: 8 -> 0, of which waited for: 8 -> 0; matrix products, arithmetic and copies ran while one was open for 11% -> 0% of each run, Pallas kernels for 0% -> 0%
where the time goes in v1:
time: 282 us; the launch traced here: 277 us
  Pallas kernels  263 us (93%)
  local copies, waits for them, and re-layouts  9 us (3%)
  other arithmetic  5.17 us (2%)
    pallas_call x2, Pallas kernels, moe_layer(): pl.pallas_call(functools.partial(layer_kernel, dims, with_norm), out_shap...  263 us
    unnamed x6, local copies, waits for them, and re-layouts  8.95 us

profile of v1, /device:TPU:33, one launch (start us, length us, event | category | flops | bytes accessed | tf_op | source)
XLA Modules:
  0.0 277.2 jit_solution(17575275428718449565)
XLA Ops:
  0.0 0.7 convert_bitcast_fusion.1
  0.7 1.3 select_maximum_fusion.1.refs_1_
  2.0 0.8 copy.13
  2.7 1.9 select_reduce_fusion
  4.6 0.1 copy.14
  4.7 1.3 select_maximum_fusion.refs_1_
  6.0 4.2 %copy.15 = bf16[256,8,2,384]{3,1,2,0:T(8,128)(2,1)} copy(bf16[256,8,2,384]{3,2,1,0:T(2,128)(2,1)} %bitcast.17) | data formatting | bytes 6291456
  10.2 0.0 copy-start
  10.2 141.2 %moe_norm.1 = (bf16[64,2048]{1,0:T(8,128)(2,1)}, bf16[64,2048]{1,0:T(8,128)(2,1)}) custom-call(bf16[64,2048]{1,0:T(8,128)(2,1)} %refs_0_.1, f32[16,128]{1,0:T(8,128)} %select_maximum_fusion.1.refs_1_, bf16[2048,768]{1,0:T(8,128)(2,1)} %bitcast.15, bf16[384,2048]{1,0:T(8,128)(2,1)} %bitcast.19, f32[1,2048]{1,0:T(1,128)} %bitcast.21), custom_call_target="tpu_custom_call" | custom-call | tf_op jit(solution)/shard_map/moe_norm/pallas_call | solution.py:340
  151.4 0.0 copy-done
  151.4 2.3 copy.16
  153.8 121.8 %moe_last.1 = bf16[64,2048]{1,0:T(8,128)(2,1)} custom-call(bf16[64,2048]{1,0:T(8,128)(2,1)} %get-tuple-element.7.refs_0_, f32[16,128]{1,0:T(8,128)} %select_maximum_fusion.refs_1_, bf16[2048,768]{1,0:T(8,128)(2,1)} %bitcast.16, bf16[384,2048]{1,0:T(8,128)(2,1)} %bitcast.20, bf16[64,2048]{1,0:T(8,128)(2,1)} %get-tuple-element.8.refs_4_), custom_call_target="tpu_custom_call" | custom-call | tf_op jit(solution)/shard_map/moe_last/pallas_call | solution.py:340
  275.5 1.7 copy.18
  (1 shorter events, 0.0 us)
Async XLA Ops:
  10.2 141.2 %copy-start = (bf16[1,2048,2,384]{3,2,1,0:T(2,128)(2,1)S(1)}, bf16[1,2048,2,384]{3,2,1,0:T(2,128)(2,1)}, u32[]{:S(2)}) copy-start(bf16[1,2048,2,384]{3,2,1,0:T(2,128)(2,1)} %param.20) | copy-start | bytes 9437188

commit v2 on v0

v2 whole, which is shorter than its diff:
```python
import functools

import jax
import jax.numpy as jnp
from jax import lax
from jax.experimental import pallas as pl
from jax.experimental.pallas import tpu as pltpu
from jax.sharding import PartitionSpec as P

F32, BF16 = jnp.float32, jnp.bfloat16
MESH = pl.DeviceIdType.MESH
PIECES = 4
LAYERS = 2


def capacity(tok_rows, top_count, expert_count):
    return max(2, min(tok_rows, 5 * tok_rows * top_count // (4 * expert_count)))


def round_up(n, unit):
    return -(-n // unit) * unit


def kernel(dims, tok_ref, ids_one, gates_one, ids_two, gates_two, place_ref, gain_ref,
           w_in_one, w_down_one, w_in_two, w_down_two, out_ref,
           ag, m_right, m_left, ct, snd, recv, hid, outs, back, rs_right, rs_left, contrib, own,
           mixed, raw, wi, wd,
           ag_s, ag_r, m_s, m_r, x_s, x_r, b_s, b_r, rs_s, rs_r, w_s, w_r, w_l, w_free):
    nz, nx, tok, width, half_ff, top, cap, rows, few, experts = dims
    steps = nz // 2
    pr = tok // PIECES
    half = PIECES // 2
    slab = nx * rows
    w_in, w_down = (w_in_one, w_in_two), (w_down_one, w_down_two)

    z, x, c = lax.axis_index("ep"), lax.axis_index("dp"), lax.axis_index("tp")
    right, left = lax.rem(z + 1, nz), lax.rem(z + nz - 1, nz)
    peers = [lax.rem(x + k, nx) for k in range(nx)]
    sources = [lax.rem(x + nx - k, nx) for k in range(nx)]

    barrier = pltpu.get_barrier_semaphore()
    pl.semaphore_signal(barrier, inc=1, device_id={"tp": 1 - c}, device_id_type=MESH)
    for index in (right, left):
        pl.semaphore_signal(barrier, inc=1, device_id={"ep": index}, device_id_type=MESH)
    for k in range(1, nx):
        pl.semaphore_signal(barrier, inc=1, device_id={"dp": peers[k]}, device_id_type=MESH)
    pl.semaphore_wait(barrier, 2 + nx)

    def remote(src, dst, send, recv_sem, axis, index):
        return pltpu.make_async_remote_copy(
            src_ref=src, dst_ref=dst, send_sem=send, recv_sem=recv_sem,
            device_id={axis: index}, device_id_type=MESH,
        )

    def cut(p, base=0):
        return pl.ds(base + p * pr, pr)

    def ring_copy(l, src, s, p, way):
        if way == 0:
            dst = ag.at[l, s, cut(p)]
        else:
            dst = ag.at[l, s, pl.ds(pl.multiple_of(jnp.where(s == steps, p * pr, tok + p * pr), pr), pr)]
        return remote(src, dst, ag_s.at[l, way, s, p], ag_r.at[l, way, s, p], "ep", (right, left)[way])

    def ring_block(l, s, p, way):
        return ag.at[l, s, cut(p, 0 if way == 0 else tok)]

    def meta_copy(src, s, way):
        return remote(src, (m_right, m_left)[way].at[s], m_s.at[way, s], m_r.at[way, s], "ep", (right, left)[way])

    def begin(l, p):
        for way in (0, 1):
            ring_copy(l, ag.at[l, 0, cut(p)], jnp.int32(1), p, way).start()

    def x_copy(l, src, dst, sems, s, k, count):
        send, recv_sem = sems
        return remote(src.at[:count], dst.at[:count], send.at[l, s, k], recv_sem.at[l, s, k], "dp", peers[k])

    def by_size(s, act):
        @pl.when(s == steps)
        def _():
            act(few)

        @pl.when(s != steps)
        def _():
            act(rows)

    def to_expert(l, s, k, n):
        return x_copy(l, snd.at[s, peers[k]], recv.at[l, s, x], (x_s, x_r), s, k, n)

    def from_owner(l, s, k, n):
        return x_copy(l, snd.at[s, sources[k]], recv.at[l, s, sources[k]], (x_s, x_r), s, k, n)

    def to_owner(l, s, k, n):
        return x_copy(l, outs.at[s, peers[k]], back.at[l, s, x], (b_s, b_r), s, k, n)

    def from_expert(l, s, k, n):
        return x_copy(l, outs.at[s, sources[k]], back.at[l, s, sources[k]], (b_s, b_r), s, k, n)

    others = range(1, nx)
    lane = lax.broadcasted_iota(jnp.int32, (8, 2 * tok), 1)
    first = (z * nx).astype(F32)

    def select(l, s):
        at = pl.ds(0, top), pl.ds(top, top)
        info = [jnp.concatenate([m_right[s, a][:, l * tok:(l + 1) * tok], m_left[s, a][:, l * tok:(l + 1) * tok]], axis=1)
                for a in at]
        ids, gates = info
        hits, values = [], []
        for k in range(nx):
            hit = ids == first + k
            hits.append(jnp.sum(jnp.where(hit, 1.0, 0.0), axis=0, keepdims=True))
            values.append(jnp.sum(jnp.where(hit, gates, 0.0), axis=0, keepdims=True))
        hit_all = jnp.concatenate(hits + [jnp.zeros((8 - nx, 2 * tok), F32)], axis=0)
        a = lax.broadcasted_iota(jnp.int32, (2 * tok, 2 * tok), 0)
        b = lax.broadcasted_iota(jnp.int32, (2 * tok, 2 * tok), 1)
        before = jnp.where((a < b) & ((a >= tok) == (b >= tok)), 1.0, 0.0).astype(BF16)
        rank = jnp.dot(hit_all.astype(BF16), before, preferred_element_type=F32)
        code = jnp.where(hit_all > 0.5, rank + jnp.where(lane >= tok, float(cap), 0.0), -1.0)
        place = lax.broadcasted_iota(jnp.int32, (rows, 2 * tok), 0).astype(F32)
        ones, weights = [], []
        for k in range(nx):
            pick = jnp.where(place == code[k:k + 1], 1.0, 0.0)
            ones.append(pick)
            weights.append(pick * values[k])
        pick = jnp.concatenate(ones, axis=0).astype(BF16)
        weight = jnp.concatenate(weights, axis=0)
        high = weight.astype(BF16)
        ct[s] = jnp.concatenate([high, (weight - high.astype(F32)).astype(BF16)], axis=1)
        chosen = jnp.dot(pick, ag[l, s], preferred_element_type=F32).astype(BF16)
        for k in range(nx):
            snd[s, k] = chosen[k * rows:(k + 1) * rows]

        def send(n):
            for k in others:
                to_expert(l, s, k, n).start()

        by_size(s, send)
        recv[l, s, x] = snd[s, x]

    def await_rows(l, s):
        def act(n):
            for k in others:
                from_owner(l, s, k, n).wait_recv()

        by_size(s, act)

    def hidden(l, s, h):
        got = jnp.concatenate([recv[l, s, k] for k in range(nx)], axis=0)
        both = jnp.dot(got, wi[h], preferred_element_type=F32)
        gate, up = both[:, :half_ff], both[:, half_ff:]
        hid[h] = (gate * (1.0 / (1.0 + jnp.exp(-gate))) * up).astype(BF16)

    def down(l, s):
        parts = [jnp.dot(hid[h], wd[h], preferred_element_type=F32).astype(BF16).astype(F32) for h in (0, 1)]
        total = (parts[0] + parts[1]).astype(BF16)
        for k in range(nx):
            outs[s, k] = total[k * rows:(k + 1) * rows]
        back[l, s, x] = outs[s, x]

    def give_back(l, s):
        def act(n):
            for k in others:
                to_owner(l, s, k, n).start()

        by_size(s, act)

    def load_in(l):
        return pltpu.make_async_copy(w_in[l].at[0], raw, w_l.at[l, 0])

    def load_down(l):
        return pltpu.make_async_copy(w_down[l].at[0], wd.at[0], w_l.at[l, 1])

    def give_in(l):
        return remote(wi.at[0], wi.at[1], w_s.at[l, 0], w_r.at[l, 0], "tp", 1 - c)

    def give_down(l):
        return remote(w_down[l].at[0], wd.at[1], w_s.at[l, 1], w_r.at[l, 1], "tp", 1 - c)

    def sort_in(p):
        part = width // PIECES
        unit = min(64, part)

        def body(i, carry):
            at = pl.ds(pl.multiple_of(p * part + i * unit, unit), unit)
            wi[0, at, :half_ff] = raw[at, 0, :]
            wi[0, at, half_ff:] = raw[at, 1, :]
            return carry

        lax.fori_loop(0, part // unit, body, 0)

    def scatter_copy(l, src, j, p, way):
        dst = (rs_right, rs_left)[way].at[l, j, cut(p)]
        return remote(src, dst, rs_s.at[l, way, j, p], rs_r.at[l, way, j, p], "ep", (right, left)[way])

    def combine(l, s):
        def act(n):
            for k in others:
                from_expert(l, s, k, n).wait_recv()

        by_size(s, act)
        got = jnp.concatenate([back[l, s, k] for k in range(nx)], axis=0)
        both = lax.dot_general(ct[s], got, (((0,), (0,)), ((), ())), preferred_element_type=F32)
        contrib[...] = both[:2 * tok] + both[2 * tok:]

    def run_layer(l):
        def gather_step(s, carry):
            moving = s <= steps - 1
            for p in range(PIECES):
                for way in (0, 1):
                    mid = (p < half) == (way == 0)
                    here = (moving & (s >= 1)) | ((s == steps) & mid)
                    onward = ((s < steps - 1) & (s >= 1)) | ((s == steps - 1) & mid)

                    @pl.when(here)
                    def _():
                        ring_copy(l, ring_block(l, 1, p, way), s, p, way).wait_recv()

                    @pl.when(onward)
                    def _():
                        ring_copy(l, ring_block(l, s, p, way), s + 1, p, way).start()
                if p == 0:
                    if l == 0:
                        @pl.when((s >= 1) & (s <= steps))
                        def _():
                            meta_copy(m_right.at[0], s, 0).wait_recv()

                        @pl.when((s >= 1) & moving)
                        def _():
                            meta_copy(m_right.at[0], s, 1).wait_recv()
                            meta_copy(m_right.at[s], s + 1, 0).start()

                        @pl.when((s >= 1) & (s < steps - 1))
                        def _():
                            meta_copy(m_left.at[s], s + 1, 1).start()

                    @pl.when((s >= 1) & (s <= steps + 1))
                    def _():
                        select(l, s - 1)
                if p == 1:
                    @pl.when(s == 1)
                    def _():
                        if l > 0:
                            pl.semaphore_wait(w_free, 1)
                            give_down(l).start()
                        give_in(l).start()

                    @pl.when(s == 2)
                    def _():
                        load_down(l).wait()
                        give_in(l).wait()
                        give_down(l).wait()

                    @pl.when(s >= 2)
                    def _():
                        await_rows(l, s - 2)
                        hidden(l, s - 2, 0)
                if p == 2:
                    @pl.when(s >= 2)
                    def _():
                        hidden(l, s - 2, 1)
                if p == 3:
                    @pl.when(s >= 2)
                    def _():
                        down(l, s - 2)

                    @pl.when(s >= steps + 1)
                    def _():
                        give_back(l, s - 2)
                @pl.when(s == 0)
                def _():
                    if p == 0:
                        load_in(l).wait()
                    sort_in(p)
            return carry

        lax.fori_loop(0, steps + 3, gather_step, 0)

        if l + 1 < LAYERS:
            pl.semaphore_signal(w_free, inc=1, device_id={"tp": 1 - c}, device_id_type=MESH)
            load_in(l + 1).start()
            load_down(l + 1).start()

        def return_rest(i, carry):
            for k in others:
                to_owner(l, steps - 2 - i, k, rows).start()
            return carry

        lax.fori_loop(0, steps - 1, return_rest, 0)

        combine(l, steps)
        for p in range(PIECES):
            way = 0 if p < half else 1
            buf = (rs_right, rs_left)[way]
            buf[l, 0, cut(p)] = contrib[cut(p)].astype(BF16)
            scatter_copy(l, buf.at[l, 0, cut(p)], 1, p, way).start()

        def scatter_step(j, carry):
            combine(l, steps - j)
            for p in range(PIECES):
                for way in (0, 1):
                    buf = (rs_right, rs_left)[way]

                    @pl.when((j >= 2) | ((p < half) == (way == 0)))
                    def _():
                        scatter_copy(l, buf.at[l, 0, cut(p)], j, p, way).wait_recv()

                    part = contrib[cut(p, tok if way == 0 else 0)]
                    buf[l, j, cut(p)] = (buf[l, j, cut(p)].astype(F32) + part).astype(BF16)
                    scatter_copy(l, buf.at[l, j, cut(p)], j + 1, p, way).start()
            return carry

        lax.fori_loop(1, steps, scatter_step, 0)

        combine(l, 0)
        own[...] = contrib[:tok]
        for p in range(PIECES):
            for way in (0, 1):
                buf = (rs_right, rs_left)[way]
                scatter_copy(l, buf.at[l, 0, cut(p)], steps, p, way).wait_recv()
            total = own[cut(p)] + rs_right[l, steps, cut(p)].astype(F32) + rs_left[l, steps, cut(p)].astype(F32)
            before = tok_ref if l == 0 else mixed
            after = (before[cut(p)].astype(F32) + total).astype(BF16)
            if l + 1 < LAYERS:
                mixed[cut(p)] = after
                wide = after.astype(F32)
                scale = lax.rsqrt(jnp.mean(wide * wide, axis=1, keepdims=True) + 1e-06)
                ag[l + 1, 0, cut(p)] = (wide * scale * gain_ref[...]).astype(BF16)
                begin(l + 1, p)
            else:
                out_ref[cut(p)] = after

        def sent(s, carry):
            for p in range(PIECES):
                for way in (0, 1):
                    mid = (p < half) == (way == 0)

                    @pl.when((s < steps) | mid)
                    def _():
                        ring_copy(l, ring_block(l, 1, p, way), s, p, way).wait_send()

                    @pl.when((s > 1) | mid)
                    def _():
                        scatter_copy(l, (rs_right, rs_left)[way].at[l, 0, cut(p)], s, p, way).wait_send()
            if l == 0:
                meta_copy(m_right.at[0], s, 0).wait_send()

                @pl.when(s < steps)
                def _():
                    meta_copy(m_right.at[0], s, 1).wait_send()
            return carry

        lax.fori_loop(1, steps + 1, sent, 0)

        def x_sent(s, carry):
            def act(n):
                for k in others:
                    to_expert(l, s, k, n).wait_send()
                    to_owner(l, s, k, n).wait_send()

            by_size(s, act)
            return carry

        lax.fori_loop(0, steps + 1, x_sent, 0)

    load_in(0).start()
    load_down(0).start()
    give_down(0).start()
    ag[0, 0, pl.ds(0, tok)] = tok_ref[...]
    for p in range(PIECES):
        for way in (0, 1):
            ring_copy(0, tok_ref.at[cut(p)], jnp.int32(1), p, way).start()
        if p == 0:
            slots = jnp.zeros(ids_two.shape, jnp.int32)
            for e in range(experts):
                slots = jnp.where(ids_two[...] == e, place_ref[e], slots)
            m_right[0, pl.ds(0, top)] = jnp.concatenate([ids_one[...], slots], axis=1).astype(F32)
            m_right[0, pl.ds(top, top)] = jnp.concatenate([gates_one[...], gates_two[...]], axis=1)
            for way in (0, 1):
                meta_copy(m_right.at[0], 1, way).start()
    nobody = jnp.full(m_left.shape[1:], -1.0, F32)
    m_left[0] = nobody
    m_left[steps] = nobody
    for l in range(LAYERS):
        ag[l, 0, pl.ds(tok, tok)] = jnp.zeros((tok, width), BF16)
        ag[l, steps, pl.ds(tok, tok)] = jnp.zeros((tok, width), BF16)
        for p in range(half, PIECES):
            rs_right[l, 1, cut(p)] = jnp.zeros((pr, width), BF16)
        for p in range(half):
            rs_left[l, 1, cut(p)] = jnp.zeros((pr, width), BF16)
        for k in range(nx):
            recv[l, steps, k, pl.ds(few, rows - few)] = jnp.zeros((rows - few, width), BF16)
            back[l, steps, k, pl.ds(few, rows - few)] = jnp.zeros((rows - few, width), BF16)
    for l in range(LAYERS):
        run_layer(l)


def moe(sizes, cap, tokens, ids_one, gates_one, ids_two, gates_two, placement, gain, w_in_one, w_down_one, w_in_two, w_down_two):
    nz, nx = sizes
    tok, width = tokens.shape
    half_ff = w_down_one.shape[1]
    top = ids_one.shape[0]
    rows, few = round_up(2 * cap, 8), round_up(cap, 8)
    dims = (nz, nx, tok, width, half_ff, top, cap, rows, few, placement.shape[0])
    groups = nz // 2 + 1
    dma = pltpu.SemaphoreType.DMA
    vmem, hbm = pl.BlockSpec(memory_space=pltpu.VMEM), pl.BlockSpec(memory_space=pl.ANY)
    smem = pl.BlockSpec(memory_space=pltpu.SMEM)
    slots = (groups, nx, rows, width)
    scratch = [
        pltpu.VMEM((LAYERS, groups, 2 * tok, width), BF16),
        pltpu.VMEM((groups, 2 * top, LAYERS * tok), F32),
        pltpu.VMEM((groups, 2 * top, LAYERS * tok), F32),
        pltpu.VMEM((groups, nx * rows, 4 * tok), BF16),
        pltpu.VMEM(slots, BF16),
        pltpu.VMEM((LAYERS, *slots), BF16),
        pltpu.VMEM((2, nx * rows, half_ff), BF16),
        pltpu.VMEM(slots, BF16),
        pltpu.VMEM((LAYERS, *slots), BF16),
        pltpu.VMEM((LAYERS, groups, tok, width), BF16),
        pltpu.VMEM((LAYERS, groups, tok, width), BF16),
        pltpu.VMEM((2 * tok, width), F32),
        pltpu.VMEM((tok, width), F32),
        pltpu.VMEM((tok, width), BF16),
        pltpu.VMEM(w_in_one.shape[1:], BF16),
        pltpu.VMEM((2, width, 2 * half_ff), BF16),
        pltpu.VMEM((2, half_ff, width), BF16),
        dma((LAYERS, 2, groups, PIECES)),
        dma((LAYERS, 2, groups, PIECES)),
        dma((2, groups)),
        dma((2, groups)),
        dma((LAYERS, groups, nx)),
        dma((LAYERS, groups, nx)),
        dma((LAYERS, groups, nx)),
        dma((LAYERS, groups, nx)),
        dma((LAYERS, 2, groups, PIECES)),
        dma((LAYERS, 2, groups, PIECES)),
        dma((LAYERS, 2)),
        dma((LAYERS, 2)),
        dma((LAYERS, 2)),
        pltpu.SemaphoreType.REGULAR,
    ]
    return pl.pallas_call(
        functools.partial(kernel, dims),
        out_shape=jax.ShapeDtypeStruct((tok, width), BF16),
        in_specs=[vmem] * 5 + [smem, vmem] + [hbm] * 4,
        out_specs=vmem,
        scratch_shapes=scratch,
        compiler_params=pltpu.CompilerParams(
            collective_id=0, has_side_effects=True, vmem_limit_bytes=63 * 1024 * 1024
        ),
        name="moe_pair",
    )(tokens, ids_one, gates_one, ids_two, gates_two, placement, gain, w_in_one, w_down_one, w_in_two, w_down_two)


def shards(sizes, tokens, experts_one, gates_one, w_in_one, w_down_one, norm_gain,
           experts_two, gates_two, placement_two, w_in_two, w_down_two):
    tok_rows, top_count = experts_one.shape
    cap = capacity(tok_rows, top_count, placement_two.shape[0])
    return moe(sizes, cap, tokens, experts_one.T, gates_one.T, experts_two.T, gates_two.T, placement_two,
               norm_gain[None, :], w_in_one, w_down_one, w_in_two, w_down_two)


def solution(mesh):
    own = P(("groups", "ep", "dp", "tp"), None)
    w_in, w_down = P(("ep", "dp"), None, None, "tp"), P(("ep", "dp"), "tp", None)
    in_specs = (own, own, own, w_in, w_down, P(), own, own, P(), w_in, w_down)
    sizes = (mesh.shape["ep"], mesh.shape["dp"])
    return jax.shard_map(functools.partial(shards, sizes), mesh=mesh, in_specs=in_specs, out_specs=own,
                         check_vma=False)
```

time: 823 us -> 259 us (0.31); the launches traced: 809 us -> 257 us
  waiting for transfers between devices: 414 us -> 0 us
  Pallas kernels: 0 us -> 256 us
  local copies, waits for them, and re-layouts: 175 us -> 1.67 us
  starting transfers between devices: 94.5 us -> 0 us
  blocking collectives: 60.6 us -> 0 us
  other arithmetic: 26.6 us -> 0 us
  matrix products: 24.5 us -> 0 us
  between operations: 14.3 us -> 0.01 us
    all_to_all x6 -> x0, waiting for transfers between devices: 349 us -> none  [the longest x2 219 us: to_owners(): lax.all_to_all(lax.all_to_all(sectioned_grid, 'dp', split_axis=1, concat_...]
    pallas_call x0 -> x1, Pallas kernels: none -> 256 us  [moe(): pl.pallas_call(functools.partial(kernel, dims), out_shape=jax.ShapeDtypeS...]
    all_to_all x6 -> x0, starting transfers between devices: 94.3 us -> none  [the longest x2 52.9 us: to_experts(): lax.all_to_all(lax.all_to_all(sectioned_grid, 'dp', split_axis=1, concat_...]
    reshape x12 -> x0, local copies, waits for them, and re-layouts: 69.1 us -> none  [the longest x2 26.9 us: rows_first(): b.reshape(-1, *t.shape[1:])]
    all_gather x2 -> x0, waiting for transfers between devices: 65 us -> none  [rows_first(): result = lax.all_gather(both, axis, axis=0, tiled=True)]
    all_to_all x2 -> x0, blocking collectives: 60.6 us -> none  [to_owners(): lax.all_to_all(sectioned_grid, 'dp', split_axis=1, concat_axis=1, tiled=T...]
    all_to_all x8 -> x0, local copies, waits for them, and re-layouts: 37 us -> none  [the longest x2 11.4 us: to_experts(): lax.all_to_all(lax.all_to_all(sectioned_grid, 'dp', split_axis=1, concat_...]
    dot_general x6 -> x0, matrix products: 24.5 us -> none  [the longest x2 12.6 us: run_expert(): jnp.dot(received, joined.reshape(row_width, 2 * full_width), preferred_el...]
  transfers between devices with their start and end apart: 8 -> 0, of which waited for: 8 -> 0; matrix products, arithmetic and copies ran while one was open for 11% -> 0% of each run, Pallas kernels for 0% -> 0%
where the time goes in v2:
time: 259 us; the launch traced here: 257 us
  Pallas kernels  256 us (99%)
    pallas_call x1, Pallas kernels, moe(): pl.pallas_call(functools.partial(kernel, dims), out_shape=jax.ShapeDtypeS...  256 us

profile of v2, /device:TPU:33, one launch (start us, length us, event | category | flops | bytes accessed | tf_op | source)
XLA Modules:
  0.0 257.4 jit_solution(14863547806898399478)
XLA Ops:
  0.0 255.7 %moe_pair.1 = bf16[64,2048]{1,0:T(8,128)(2,1)} custom-call(bf16[64,2048]{1,0:T(8,128)(2,1)} %tok_ref.1, s32[8,64]{1,0:T(8,128)} %bitcast.6, f32[8,64]{1,0:T(8,128)} %bitcast.7, s32[8,64]{1,0:T(8,128)} %bitcast.8, f32[8,64]{1,0:T(8,128)} %bitcast.9, s32[64]{0:T(128)} %place_ref.1, f32[1,2048]{1,0:T(1,128)} %bitcast.5, bf16[1,2048,2,384]{3,2,1,0:T(2,128)(2,1)} %w_in_one.1, ...), custom_call_target="tpu_custom_call" | custom-call | tf_op jit(solution)/shard_map/moe_pair/pallas_call | solution.py:443
  255.7 1.7 copy.13

commit v3 on v2

--- a/solution.py
+++ b/solution.py
@@ -11,6 +11,7 @@
 MESH = pl.DeviceIdType.MESH
 PIECES = 4
 LAYERS = 2
+HEAD_START = 4
 
 
 def capacity(tok_rows, top_count, expert_count):
@@ -25,11 +26,13 @@
            w_in_one, w_down_one, w_in_two, w_down_two, out_ref,
            ag, m_right, m_left, ct, snd, recv, hid, outs, back, rs_right, rs_left, contrib, own,
            mixed, raw, wi, wd,
-           ag_s, ag_r, m_s, m_r, x_s, x_r, b_s, b_r, rs_s, rs_r, w_s, w_r, w_l, w_free):
+           ag_s, ag_r, m_s, m_r, x_s, x_r, b_s, b_r, rs_s, rs_r, w_s, w_r, w_l, w_free, go):
     nz, nx, tok, width, half_ff, top, cap, rows, few, experts = dims
     steps = nz // 2
     pr = tok // PIECES
     half = PIECES // 2
+    sort_steps = min(4, steps - 1)
+    head_start = min(HEAD_START, steps)
     slab = nx * rows
     w_in, w_down = (w_in_one, w_in_two), (w_down_one, w_down_two)
 
@@ -149,10 +152,10 @@
         got = jnp.concatenate([recv[l, s, k] for k in range(nx)], axis=0)
         both = jnp.dot(got, wi[h], preferred_element_type=F32)
         gate, up = both[:, :half_ff], both[:, half_ff:]
-        hid[h] = (gate * (1.0 / (1.0 + jnp.exp(-gate))) * up).astype(BF16)
+        hid[lax.rem(s, 2), h] = (gate * (1.0 / (1.0 + jnp.exp(-gate))) * up).astype(BF16)
 
     def down(l, s):
-        parts = [jnp.dot(hid[h], wd[h], preferred_element_type=F32).astype(BF16).astype(F32) for h in (0, 1)]
+        parts = [jnp.dot(hid[lax.rem(s, 2), h], wd[h], preferred_element_type=F32).astype(BF16).astype(F32) for h in (0, 1)]
         total = (parts[0] + parts[1]).astype(BF16)
         for k in range(nx):
             outs[s, k] = total[k * rows:(k + 1) * rows]
@@ -177,17 +180,20 @@
     def give_down(l):
         return remote(w_down[l].at[0], wd.at[1], w_s.at[l, 1], w_r.at[l, 1], "tp", 1 - c)
 
-    def sort_in(p):
-        part = width // PIECES
-        unit = min(64, part)
+    def sort_in(i):
+        unit = width // (sort_steps * PIECES)
+        at = pl.ds(pl.multiple_of(i * unit, unit), unit)
+        wi[0, at, :half_ff] = raw[at, 0, :]
+        wi[0, at, half_ff:] = raw[at, 1, :]
+
+    def sort_all(l):
+        load_in(l).wait()
 
         def body(i, carry):
-            at = pl.ds(pl.multiple_of(p * part + i * unit, unit), unit)
-            wi[0, at, :half_ff] = raw[at, 0, :]
-            wi[0, at, half_ff:] = raw[at, 1, :]
+            sort_in(i)
             return carry
 
-        lax.fori_loop(0, part // unit, body, 0)
+        lax.fori_loop(0, sort_steps * PIECES, body, 0)
 
     def scatter_copy(l, src, j, p, way):
         dst = (rs_right, rs_left)[way].at[l, j, cut(p)]
@@ -204,6 +210,23 @@
         contrib[...] = both[:2 * tok] + both[2 * tok:]
 
     def run_layer(l):
+        ready = jnp.where(c == 1, 2, sort_steps + 1) if l == 0 else min(3, steps)
+
+        def bound(s):
+            at = jnp.where(s == steps + 1, steps, s)
+            return jnp.where(at <= ready, 0, jnp.minimum(2 * (at - ready), at - 2))
+
+        def each_group(s, act):
+            def body(g, carry):
+                act(g)
+                return carry
+
+            lax.fori_loop(bound(s), bound(s + 1), body, 0)
+
+        def first_half(g):
+            await_rows(l, g)
+            hidden(l, g, 0)
+
         def gather_step(s, carry):
             moving = s <= steps - 1
             for p in range(PIECES):
@@ -234,59 +257,64 @@
                         def _():
                             meta_copy(m_left.at[s], s + 1, 1).start()
 
+                        @pl.when((s == head_start) & (c == 0))
+                        def _():
+                            pl.semaphore_signal(go, inc=1, device_id={"tp": 1 - c}, device_id_type=MESH)
+
+                        @pl.when((s == sort_steps) & (c == 0))
+                        def _():
+                            give_in(0).start()
+                            load_in(1).start()
+                    else:
+                        @pl.when((s == 1) & (c == 0))
+                        def _():
+                            pl.semaphore_wait(w_free, 1)
+                            give_down(l).start()
+                            give_in(l).start()
+
                     @pl.when((s >= 1) & (s <= steps + 1))
                     def _():
                         select(l, s - 1)
                 if p == 1:
-                    @pl.when(s == 1)
-                    def _():
-                        if l > 0:
-                            pl.semaphore_wait(w_free, 1)
-                            give_down(l).start()
-                        give_in(l).start()
-
-                    @pl.when(s == 2)
+                    @pl.when(s == ready)
                     def _():
                         load_down(l).wait()
                         give_in(l).wait()
                         give_down(l).wait()
 
-                    @pl.when(s >= 2)
-                    def _():
-                        await_rows(l, s - 2)
-                        hidden(l, s - 2, 0)
+                    each_group(s, first_half)
                 if p == 2:
-                    @pl.when(s >= 2)
-                    def _():
-                        hidden(l, s - 2, 1)
+                    each_group(s, lambda g: hidden(l, g, 1))
                 if p == 3:
-                    @pl.when(s >= 2)
-                    def _():
-                        down(l, s - 2)
-
-                    @pl.when(s >= steps + 1)
-                    def _():
-                        give_back(l, s - 2)
-                @pl.when(s == 0)
-                def _():
-                    if p == 0:
-                        load_in(l).wait()
-                    sort_in(p)
+                    each_group(s, lambda g: down(l, g))
+                if l == 0:
+                    @pl.when((s < sort_steps) & (c == 0))
+                    def _():
+                        if p == 0:
+                            @pl.when(s == 0)
+                            def _():
+                                load_in(0).wait()
+                        sort_in(s * PIECES + p)
             return carry
 
         lax.fori_loop(0, steps + 3, gather_step, 0)
+
+        def return_rows(i, carry):
+            give_back(l, steps - i)
+            return carry
+
+        lax.fori_loop(0, steps + 1, return_rows, 0)
 
         if l + 1 < LAYERS:
             pl.semaphore_signal(w_free, inc=1, device_id={"tp": 1 - c}, device_id_type=MESH)
-            load_in(l + 1).start()
             load_down(l + 1).start()
-
-        def return_rest(i, carry):
-            for k in others:
-                to_owner(l, steps - 2 - i, k, rows).start()
-            return carry
-
-        lax.fori_loop(0, steps - 1, return_rest, 0)
+            sort_all(l + 1)
+
+            @pl.when(c == 1)
+            def _():
+                pl.semaphore_wait(w_free, 1)
+                give_down(l + 1).start()
+                give_in(l + 1).start()
 
         combine(l, steps)
         for p in range(PIECES):
@@ -367,17 +395,19 @@
     load_down(0).start()
     give_down(0).start()
     ag[0, 0, pl.ds(0, tok)] = tok_ref[...]
-    for p in range(PIECES):
-        for way in (0, 1):
-            ring_copy(0, tok_ref.at[cut(p)], jnp.int32(1), p, way).start()
-        if p == 0:
-            slots = jnp.zeros(ids_two.shape, jnp.int32)
-            for e in range(experts):
-                slots = jnp.where(ids_two[...] == e, place_ref[e], slots)
-            m_right[0, pl.ds(0, top)] = jnp.concatenate([ids_one[...], slots], axis=1).astype(F32)
-            m_right[0, pl.ds(top, top)] = jnp.concatenate([gates_one[...], gates_two[...]], axis=1)
-            for way in (0, 1):
-                meta_copy(m_right.at[0], 1, way).start()
+
+    @pl.when(c == 0)
+    def _():
+        for p in range(PIECES):
+            begin(0, p)
+
+    slots = jnp.zeros(ids_two.shape, jnp.int32)
+    for e in range(experts):
+        slots = jnp.where(ids_two[...] == e, place_ref[e], slots)
+    m_right[0, pl.ds(0, top)] = jnp.concatenate([ids_one[...], slots], axis=1).astype(F32)
+    m_right[0, pl.ds(top, top)] = jnp.concatenate([gates_one[...], gates_two[...]], axis=1)
+    for way in (0, 1):
+        meta_copy(m_right.at[0], 1, way).start()
     nobody = jnp.full(m_left.shape[1:], -1.0, F32)
     m_left[0] = nobody
     m_left[steps] = nobody
@@ -391,6 +421,16 @@
         for k in range(nx):
             recv[l, steps, k, pl.ds(few, rows - few)] = jnp.zeros((rows - few, width), BF16)
             back[l, steps, k, pl.ds(few, rows - few)] = jnp.zeros((rows - few, width), BF16)
+
+    @pl.when(c == 1)
+    def _():
+        sort_all(0)
+        give_in(0).start()
+        load_in(1).start()
+        pl.semaphore_wait(go, 1)
+        for p in range(PIECES):
+            begin(0, p)
+
     for l in range(LAYERS):
         run_layer(l)
 
@@ -414,7 +454,7 @@
         pltpu.VMEM((groups, nx * rows, 4 * tok), BF16),
         pltpu.VMEM(slots, BF16),
         pltpu.VMEM((LAYERS, *slots), BF16),
-        pltpu.VMEM((2, nx * rows, half_ff), BF16),
+        pltpu.VMEM((2, 2, nx * rows, half_ff), BF16),
         pltpu.VMEM(slots, BF16),
         pltpu.VMEM((LAYERS, *slots), BF16),
         pltpu.VMEM((LAYERS, groups, tok, width), BF16),
@@ -439,6 +479,7 @@
         dma((LAYERS, 2)),
         dma((LAYERS, 2)),
         pltpu.SemaphoreType.REGULAR,
+        pltpu.SemaphoreType.REGULAR,
     ]
     return pl.pallas_call(
         functools.partial(kernel, dims),

time: 259 us -> 247 us (0.954)
  Pallas kernels: 256 us -> 245 us
    pallas_call x1, Pallas kernels: 256 us -> 245 us  [moe(): pl.pallas_call(functools.partial(kernel, dims), out_shape=jax.ShapeDtypeS...]
where the time goes in v3:
time: 247 us
  Pallas kernels  245 us (99%)
    pallas_call x1, Pallas kernels, moe(): pl.pallas_call(functools.partial(kernel, dims), out_shape=jax.ShapeDtypeS...  245 us

profile of v3, /device:TPU:33, one launch (start us, length us, event | category | flops | bytes accessed | tf_op | source)
XLA Modules:
  0.0 247.1 jit_solution(8200718594497414249)
XLA Ops:
  0.0 245.4 %moe_pair.1 = bf16[64,2048]{1,0:T(8,128)(2,1)} custom-call(bf16[64,2048]{1,0:T(8,128)(2,1)} %tok_ref.1, s32[8,64]{1,0:T(8,128)} %bitcast.6, f32[8,64]{1,0:T(8,128)} %bitcast.7, s32[8,64]{1,0:T(8,128)} %bitcast.8, f32[8,64]{1,0:T(8,128)} %bitcast.9, s32[64]{0:T(128)} %place_ref.1, f32[1,2048]{1,0:T(1,128)} %bitcast.5, bf16[1,2048,2,384]{3,2,1,0:T(2,128)(2,1)} %w_in_one.1, ...), custom_call_target="tpu_custom_call" | custom-call | tf_op jit(solution)/shard_map/moe_pair/pallas_call | solution.py:484
  245.4 1.7 copy.13

commit v4 on v3

--- a/solution.py
+++ b/solution.py
@@ -11,7 +11,8 @@
 MESH = pl.DeviceIdType.MESH
 PIECES = 4
 LAYERS = 2
-HEAD_START = 4
+HEAD_START = 3
+FIRST = 0
 
 
 def capacity(tok_rows, top_count, expert_count):
@@ -39,7 +40,6 @@
     z, x, c = lax.axis_index("ep"), lax.axis_index("dp"), lax.axis_index("tp")
     right, left = lax.rem(z + 1, nz), lax.rem(z + nz - 1, nz)
     peers = [lax.rem(x + k, nx) for k in range(nx)]
-    sources = [lax.rem(x + nx - k, nx) for k in range(nx)]
 
     barrier = pltpu.get_barrier_semaphore()
     pl.semaphore_signal(barrier, inc=1, device_id={"tp": 1 - c}, device_id_type=MESH)
@@ -63,21 +63,30 @@
             dst = ag.at[l, s, cut(p)]
         else:
             dst = ag.at[l, s, pl.ds(pl.multiple_of(jnp.where(s == steps, p * pr, tok + p * pr), pr), pr)]
-        return remote(src, dst, ag_s.at[l, way, s, p], ag_r.at[l, way, s, p], "ep", (right, left)[way])
+        return remote(src, dst, ag_s.at[way, s], ag_r.at[way, s, p], "ep", (right, left)[way])
 
     def ring_block(l, s, p, way):
         return ag.at[l, s, cut(p, 0 if way == 0 else tok)]
 
+    def ring_sent(l, s, way, count):
+        return remote(ag.at[l, 1, :count], ag.at[l, 1, :count], ag_s.at[way, s], ag_r.at[way, s, 0], "ep", (right, left)[way])
+
+    def scatter_block(l, j, way, count):
+        buf = (rs_right, rs_left)[way]
+        return remote(buf.at[l, 1, :count], buf.at[l, 1, :count], rs_s.at[way, j], rs_r.at[way, j, 0], "ep", (right, left)[way])
+
     def meta_copy(src, s, way):
-        return remote(src, (m_right, m_left)[way].at[s], m_s.at[way, s], m_r.at[way, s], "ep", (right, left)[way])
+        return remote(src, (m_right, m_left)[way].at[s], m_s.at[way], m_r.at[way, s], "ep", (right, left)[way])
 
     def begin(l, p):
         for way in (0, 1):
             ring_copy(l, ag.at[l, 0, cut(p)], jnp.int32(1), p, way).start()
 
-    def x_copy(l, src, dst, sems, s, k, count):
-        send, recv_sem = sems
-        return remote(src.at[:count], dst.at[:count], send.at[l, s, k], recv_sem.at[l, s, k], "dp", peers[k])
+    def x_copy(src, dst, sems, s, k, count):
+        return remote(src.at[:count], dst.at[:count], sems[0].at[s], sems[1].at[s], "dp", peers[k])
+
+    def x_all(l, sems, s, count):
+        return remote(snd.at[s, :nx - 1, :count], recv.at[l, s, :nx - 1, :count], sems[0].at[s], sems[1].at[s], "dp", peers[1])
 
     def by_size(s, act):
         @pl.when(s == steps)
@@ -89,16 +98,10 @@
             act(rows)
 
     def to_expert(l, s, k, n):
-        return x_copy(l, snd.at[s, peers[k]], recv.at[l, s, x], (x_s, x_r), s, k, n)
-
-    def from_owner(l, s, k, n):
-        return x_copy(l, snd.at[s, sources[k]], recv.at[l, s, sources[k]], (x_s, x_r), s, k, n)
+        return x_copy(snd.at[s, peers[k]], recv.at[l, s, x], (x_s, x_r), s, k, n)
 
     def to_owner(l, s, k, n):
-        return x_copy(l, outs.at[s, peers[k]], back.at[l, s, x], (b_s, b_r), s, k, n)
-
-    def from_expert(l, s, k, n):
-        return x_copy(l, outs.at[s, sources[k]], back.at[l, s, sources[k]], (b_s, b_r), s, k, n)
+        return x_copy(outs.at[s, peers[k]], back.at[l, s, x], (b_s, b_r), s, k, n)
 
     others = range(1, nx)
     lane = lax.broadcasted_iota(jnp.int32, (8, 2 * tok), 1)
@@ -142,11 +145,7 @@
         recv[l, s, x] = snd[s, x]
 
     def await_rows(l, s):
-        def act(n):
-            for k in others:
-                from_owner(l, s, k, n).wait_recv()
-
-        by_size(s, act)
+        by_size(s, lambda n: x_all(l, (x_s, x_r), s, n).wait_recv())
 
     def hidden(l, s, h):
         got = jnp.concatenate([recv[l, s, k] for k in range(nx)], axis=0)
@@ -169,16 +168,16 @@
         by_size(s, act)
 
     def load_in(l):
-        return pltpu.make_async_copy(w_in[l].at[0], raw, w_l.at[l, 0])
+        return pltpu.make_async_copy(w_in[l].at[0], raw, w_l.at[0])
 
     def load_down(l):
-        return pltpu.make_async_copy(w_down[l].at[0], wd.at[0], w_l.at[l, 1])
+        return pltpu.make_async_copy(w_down[l].at[0], wd.at[0], w_l.at[1])
 
     def give_in(l):
-        return remote(wi.at[0], wi.at[1], w_s.at[l, 0], w_r.at[l, 0], "tp", 1 - c)
+        return remote(wi.at[0], wi.at[1], w_s.at[0], w_r.at[0], "tp", 1 - c)
 
     def give_down(l):
-        return remote(w_down[l].at[0], wd.at[1], w_s.at[l, 1], w_r.at[l, 1], "tp", 1 - c)
+        return remote(w_down[l].at[0], wd.at[1], w_s.at[1], w_r.at[1], "tp", 1 - c)
 
     def sort_in(i):
         unit = width // (sort_steps * PIECES)
@@ -197,20 +196,16 @@
 
     def scatter_copy(l, src, j, p, way):
         dst = (rs_right, rs_left)[way].at[l, j, cut(p)]
-        return remote(src, dst, rs_s.at[l, way, j, p], rs_r.at[l, way, j, p], "ep", (right, left)[way])
+        return remote(src, dst, rs_s.at[way, j], rs_r.at[way, j, p], "ep", (right, left)[way])
 
     def combine(l, s):
-        def act(n):
-            for k in others:
-                from_expert(l, s, k, n).wait_recv()
-
-        by_size(s, act)
+        by_size(s, lambda n: x_all(l, (b_s, b_r), s, n).wait_recv())
         got = jnp.concatenate([back[l, s, k] for k in range(nx)], axis=0)
         both = lax.dot_general(ct[s], got, (((0,), (0,)), ((), ())), preferred_element_type=F32)
         contrib[...] = both[:2 * tok] + both[2 * tok:]
 
     def run_layer(l):
-        ready = jnp.where(c == 1, 2, sort_steps + 1) if l == 0 else min(3, steps)
+        ready = jnp.where(c != FIRST, 2, sort_steps + 1) if l == 0 else min(3, steps)
 
         def bound(s):
             at = jnp.where(s == steps + 1, steps, s)
@@ -244,29 +239,16 @@
                         ring_copy(l, ring_block(l, s, p, way), s + 1, p, way).start()
                 if p == 0:
                     if l == 0:
-                        @pl.when((s >= 1) & (s <= steps))
-                        def _():
-                            meta_copy(m_right.at[0], s, 0).wait_recv()
-
-                        @pl.when((s >= 1) & moving)
-                        def _():
-                            meta_copy(m_right.at[0], s, 1).wait_recv()
-                            meta_copy(m_right.at[s], s + 1, 0).start()
-
-                        @pl.when((s >= 1) & (s < steps - 1))
-                        def _():
-                            meta_copy(m_left.at[s], s + 1, 1).start()
-
-                        @pl.when((s == head_start) & (c == 0))
+                        @pl.when((s == head_start) & (c == FIRST))
                         def _():
                             pl.semaphore_signal(go, inc=1, device_id={"tp": 1 - c}, device_id_type=MESH)
 
-                        @pl.when((s == sort_steps) & (c == 0))
+                        @pl.when((s == sort_steps) & (c == FIRST))
                         def _():
                             give_in(0).start()
                             load_in(1).start()
                     else:
-                        @pl.when((s == 1) & (c == 0))
+                        @pl.when((s == 1) & (c == FIRST))
                         def _():
                             pl.semaphore_wait(w_free, 1)
                             give_down(l).start()
@@ -286,9 +268,23 @@
                 if p == 2:
                     each_group(s, lambda g: hidden(l, g, 1))
                 if p == 3:
+                    if l == 0:
+                        @pl.when((s >= 1) & (s <= steps))
+                        def _():
+                            meta_copy(m_right.at[0], s, 0).wait_recv()
+
+                        @pl.when((s >= 1) & moving)
+                        def _():
+                            meta_copy(m_right.at[0], s, 1).wait_recv()
+                            meta_copy(m_right.at[s], s + 1, 0).start()
+
+                        @pl.when((s >= 1) & (s < steps - 1))
+                        def _():
+                            meta_copy(m_left.at[s], s + 1, 1).start()
+
                     each_group(s, lambda g: down(l, g))
                 if l == 0:
-                    @pl.when((s < sort_steps) & (c == 0))
+                    @pl.when((s < sort_steps) & (c == FIRST))
                     def _():
                         if p == 0:
                             @pl.when(s == 0)
@@ -305,16 +301,26 @@
 
         lax.fori_loop(0, steps + 1, return_rows, 0)
 
+        def gathered(s, carry):
+            for way in (0, 1):
+                ring_sent(l, s, way, tok).wait_send()
+            return carry
+
+        def chosen_sent(s, carry):
+            by_size(s, lambda n: x_all(l, (x_s, x_r), s, n).wait_send())
+            return carry
+
+        lax.fori_loop(1, steps, gathered, 0)
+        for way in (0, 1):
+            ring_sent(l, steps, way, tok // 2).wait_send()
+        lax.fori_loop(0, steps + 1, chosen_sent, 0)
+        if l == 0:
+            remote(m_right.at[:steps], m_right.at[:steps], m_s.at[0], m_r.at[0, 1], "ep", right).wait_send()
+            remote(m_left.at[:steps - 1], m_left.at[:steps - 1], m_s.at[1], m_r.at[1, 1], "ep", left).wait_send()
+
         if l + 1 < LAYERS:
             pl.semaphore_signal(w_free, inc=1, device_id={"tp": 1 - c}, device_id_type=MESH)
             load_down(l + 1).start()
-            sort_all(l + 1)
-
-            @pl.when(c == 1)
-            def _():
-                pl.semaphore_wait(w_free, 1)
-                give_down(l + 1).start()
-                give_in(l + 1).start()
 
         combine(l, steps)
         for p in range(PIECES):
@@ -326,6 +332,21 @@
         def scatter_step(j, carry):
             combine(l, steps - j)
             for p in range(PIECES):
+                if l + 1 < LAYERS:
+                    @pl.when(j <= sort_steps)
+                    def _():
+                        if p == 0:
+                            @pl.when(j == 1)
+                            def _():
+                                load_in(l + 1).wait()
+                        sort_in((j - 1) * PIECES + p)
+
+                    if p == PIECES - 1:
+                        @pl.when((j == sort_steps) & (c != FIRST))
+                        def _():
+                            pl.semaphore_wait(w_free, 1)
+                            give_down(l + 1).start()
+                            give_in(l + 1).start()
                 for way in (0, 1):
                     buf = (rs_right, rs_left)[way]
 
@@ -358,45 +379,27 @@
             else:
                 out_ref[cut(p)] = after
 
-        def sent(s, carry):
-            for p in range(PIECES):
-                for way in (0, 1):
-                    mid = (p < half) == (way == 0)
-
-                    @pl.when((s < steps) | mid)
-                    def _():
-                        ring_copy(l, ring_block(l, 1, p, way), s, p, way).wait_send()
-
-                    @pl.when((s > 1) | mid)
-                    def _():
-                        scatter_copy(l, (rs_right, rs_left)[way].at[l, 0, cut(p)], s, p, way).wait_send()
-            if l == 0:
-                meta_copy(m_right.at[0], s, 0).wait_send()
-
-                @pl.when(s < steps)
-                def _():
-                    meta_copy(m_right.at[0], s, 1).wait_send()
-            return carry
-
-        lax.fori_loop(1, steps + 1, sent, 0)
-
-        def x_sent(s, carry):
-            def act(n):
-                for k in others:
-                    to_expert(l, s, k, n).wait_send()
-                    to_owner(l, s, k, n).wait_send()
-
-            by_size(s, act)
-            return carry
-
-        lax.fori_loop(0, steps + 1, x_sent, 0)
+        def scattered(j, carry):
+            for way in (0, 1):
+                scatter_block(l, j, way, tok).wait_send()
+            return carry
+
+        for way in (0, 1):
+            scatter_block(l, 1, way, tok // 2).wait_send()
+        lax.fori_loop(2, steps + 1, scattered, 0)
+
+        def returned(s, carry):
+            by_size(s, lambda n: x_all(l, (b_s, b_r), s, n).wait_send())
+            return carry
+
+        lax.fori_loop(0, steps + 1, returned, 0)
 
     load_in(0).start()
     load_down(0).start()
     give_down(0).start()
     ag[0, 0, pl.ds(0, tok)] = tok_ref[...]
 
-    @pl.when(c == 0)
+    @pl.when(c == FIRST)
     def _():
         for p in range(PIECES):
             begin(0, p)
@@ -422,7 +425,7 @@
             recv[l, steps, k, pl.ds(few, rows - few)] = jnp.zeros((rows - few, width), BF16)
             back[l, steps, k, pl.ds(few, rows - few)] = jnp.zeros((rows - few, width), BF16)
 
-    @pl.when(c == 1)
+    @pl.when(c != FIRST)
     def _():
         sort_all(0)
         give_in(0).start()
@@ -465,19 +468,19 @@
         pltpu.VMEM(w_in_one.shape[1:], BF16),
         pltpu.VMEM((2, width, 2 * half_ff), BF16),
         pltpu.VMEM((2, half_ff, width), BF16),
-        dma((LAYERS, 2, groups, PIECES)),
-        dma((LAYERS, 2, groups, PIECES)),
         dma((2, groups)),
+        dma((2, groups, PIECES)),
+        dma((2,)),
         dma((2, groups)),
-        dma((LAYERS, groups, nx)),
-        dma((LAYERS, groups, nx)),
-        dma((LAYERS, groups, nx)),
-        dma((LAYERS, groups, nx)),
-        dma((LAYERS, 2, groups, PIECES)),
-        dma((LAYERS, 2, groups, PIECES)),
-        dma((LAYERS, 2)),
-        dma((LAYERS, 2)),
-        dma((LAYERS, 2)),
+        dma((groups,)),
+        dma((groups,)),
+        dma((groups,)),
+        dma((groups,)),
+        dma((2, groups)),
+        dma((2, groups, PIECES)),
+        dma((2,)),
+        dma((2,)),
+        dma((2,)),
         pltpu.SemaphoreType.REGULAR,
         pltpu.SemaphoreType.REGULAR,
     ]

time: 247 us -> 240 us (0.972)
  Pallas kernels: 245 us -> 238 us
    pallas_call x1, Pallas kernels: 245 us -> 238 us  [moe(): pl.pallas_call(functools.partial(kernel, dims), out_shape=jax.ShapeDtypeS...]
where the time goes in v4:
time: 240 us
  Pallas kernels  238 us (99%)
    pallas_call x1, Pallas kernels, moe(): pl.pallas_call(functools.partial(kernel, dims), out_shape=jax.ShapeDtypeS...  238 us

profile of v4, /device:TPU:33, one launch (start us, length us, event | category | flops | bytes accessed | tf_op | source)
XLA Modules:
  0.0 240.1 jit_solution(1645207560324227621)
XLA Ops:
  0.0 238.4 %moe_pair.1 = bf16[64,2048]{1,0:T(8,128)(2,1)} custom-call(bf16[64,2048]{1,0:T(8,128)(2,1)} %tok_ref.1, s32[8,64]{1,0:T(8,128)} %bitcast.6, f32[8,64]{1,0:T(8,128)} %bitcast.7, s32[8,64]{1,0:T(8,128)} %bitcast.8, f32[8,64]{1,0:T(8,128)} %bitcast.9, s32[64]{0:T(128)} %place_ref.1, f32[1,2048]{1,0:T(1,128)} %bitcast.5, bf16[1,2048,2,384]{3,2,1,0:T(2,128)(2,1)} %w_in_one.1, ...), custom_call_target="tpu_custom_call" | custom-call | tf_op jit(solution)/shard_map/moe_pair/pallas_call | solution.py:487
  238.4 1.7 copy.13
